TPU v7x, 256 devices: a whole 4x4x8 slice. The times are simulated.
256 devices in a mesh: pair: 32 (over y, x, core), sec: 8 (over z).
Axes of the slice: x: 4, y: 4, z: 8, core: 2. Of those that a mesh axis runs over, the one named last changes fastest.
Arguments:
- source: float32 [16384, 4096], P('sec', 'pair'), may hold values from -6 to 6
- occ_energy: float32 [4096], P('pair'), may hold values from 0.5 to 2
- virt_energy: float32 [16384], P('sec'), may hold values from 0.5 to 2
- v_tiles: float32 [256, 256, 256], P('sec'), may hold values from -0.12 to 0.12
- v_rows: int32 [256], P('sec'), may hold values from 0 to 11, as said below
- v_cols: int32 [256], P('sec'), may hold values from 0 to 7
- v_count: int32 [8], P('sec'), may hold values from 8 to 32, as said below
- w_tiles: float32 [48, 128, 128], replicated, may hold values from -0.18 to 0.18
- w_rows: int32 [48], replicated, may hold values from 0 to 31, as said below
- w_cols: int32 [48], replicated, may hold values from 0 to 31, as said below
Outputs:
- amplitudes: float32 [16384, 4096], P('sec', 'pair')
Inputs may be any that keep to these rules, and one draw needn't show every extreme that they name: Entry n belongs to section s = n // 32; its row tile s * 8 - 2 + v_rows[n] lies inside the virtual range and differs from its column tile by at most 2. In every section but the first some used entry has v_rows 0 and some has 1; in every section but the last some used entry has 10 and some has 11. Only the first v_count[s] entries of section s are used; one section uses all 32, every other one at most 16. `w_rows`: every tile index appears; a pair may repeat, and repeated tiles add. `w_cols`: every tile index appears.
All inputs are finite; a program needn't handle non-finite values.
Results may differ from a plain program's by a relative error of at most 0.0003.
Values sent between devices are 32-bit elements; how exact they have to be, the bound alone decides.
A program may use at most 128 MiB of HBM per device.

v0:
```python
import functools

import jax
import jax.numpy as jnp
from jax import lax
from jax.experimental import pallas as pl
from jax.experimental.pallas import tpu as pltpu
from jax.sharding import PartitionSpec as P

MESH = pl.DeviceIdType.MESH
VT = 256
OT = 128
REACH = 2
SPAN = 2 * REACH + 1
F32 = jnp.float32
BF16 = jnp.bfloat16


def split(x):
    high = x.astype(BF16)
    low = (x - high.astype(F32)).astype(BF16)
    return high, low


def tables_kernel(v_rows, v_cols, v_count, w_rows, last_v, prev_v, last_w, prev_w):
    slots, section = v_rows.shape[0], last_v.shape[0] // SPAN
    wslots, tiles = w_rows.shape[0], last_w.shape[0]

    @pl.loop(0, section * SPAN)
    def _(i):
        last_v[i] = slots

    @pl.loop(0, tiles)
    def _(i):
        last_w[i] = wslots

    @pl.loop(0, slots)
    def _(n):
        prev_v[n] = slots

    @pl.loop(0, v_count[0])
    def _(n):
        key = v_cols[n] * SPAN + v_rows[n] - v_cols[n]
        prev_v[n] = last_v[key]
        last_v[key] = n

    @pl.loop(0, wslots)
    def _(n):
        key = w_rows[n]
        prev_w[n] = last_w[key]
        last_w[key] = n


def tables(v_rows, v_cols, v_count, w_rows, section, tiles):
    smem = pl.BlockSpec(memory_space=pltpu.SMEM)
    i32 = lambda n: jax.ShapeDtypeStruct((n,), jnp.int32)
    return pl.pallas_call(
        tables_kernel,
        out_shape=(i32(section * SPAN), i32(v_rows.shape[0]), i32(tiles), i32(w_rows.shape[0])),
        in_specs=[smem] * 4,
        out_specs=(smem,) * 4,
        name="tables",
    )(v_rows, v_cols, v_count, w_rows)


def far_first():
    steps = [(dx, dy, dc) for dx in range(-1, 3) for dy in range(-1, 3) for dc in range(2)]
    steps.remove((0, 0, 0))
    return sorted(steps, key=lambda s: -abs(s[0]) - abs(s[1]))


def partners(me, count):
    if count != 32:
        return [lax.rem(me + k, count) for k in range(1, count)]
    y, x, c = lax.div(me, 8), lax.rem(lax.div(me, 2), 4), lax.rem(me, 2)
    return [
        lax.rem(y + dy + 4, 4) * 8 + lax.rem(x + dx + 4, 4) * 2 + lax.rem(c + dc, 2)
        for dx, dy, dc in far_first()
    ]


def kernel(
    count,
    sections,
    last_v,
    prev_v,
    last_w,
    prev_w,
    w_cols,
    source,
    occ,
    virt,
    v_tiles,
    w_tiles,
    out,
    s_buf,
    occ_own,
    occ_all,
    virt_rows,
    virt_wide,
    v_stage,
    w_stage,
    v_split,
    w_split,
    start_a,
    scale_a,
    start_b,
    scale_b,
    part_a,
    part_b,
    hole_b,
    hole_a,
    window,
    split_b,
    chain,
    edge,
    halo,
    load_sem,
    v_sem,
    occ_sem,
    send_sem,
    recv_sem,
    edge_sem,
    halo_sem,
):
    rows = source.shape[0]
    block = rows // count
    section = rows // VT
    slots = v_tiles.shape[0] // VT
    wslots = w_tiles.shape[0] // OT
    groups = v_sem.shape[0]
    per_group = slots // groups
    me = lax.axis_index("pair")
    z = lax.axis_index("sec")
    up, down = lax.rem(z + 1, sections), lax.rem(z + sections - 1, sections)

    loads = [
        pltpu.make_async_copy(source, s_buf, load_sem.at[0]),
        pltpu.make_async_copy(occ, occ_own, load_sem.at[1]),
        pltpu.make_async_copy(virt, virt_rows, load_sem.at[2]),
    ]
    for copy in loads:
        copy.start()
    v_loads = []
    for g in range(groups):
        part = pl.ds(g * per_group * VT, per_group * VT)
        v_loads.append(pltpu.make_async_copy(v_tiles.at[part], v_stage.at[part], v_sem.at[g]))
        v_loads[-1].start()
    w_load = pltpu.make_async_copy(w_tiles, w_stage, load_sem.at[3])
    w_load.start()

    barrier = pltpu.get_barrier_semaphore()

    @pl.loop(1, count)
    def _(k):
        pl.semaphore_signal(
            barrier, inc=1, device_id={"pair": lax.rem(me + k, count)}, device_id_type=MESH
        )

    pl.semaphore_signal(barrier, inc=1, device_id={"sec": up}, device_id_type=MESH)
    pl.semaphore_signal(barrier, inc=1, device_id={"sec": down}, device_id_type=MESH)

    v_split[slots] = jnp.zeros((2, VT, VT), BF16)
    chain[wslots] = jnp.zeros((block, OT), F32)

    def blk(d):
        return pl.ds(pl.multiple_of(d * block, block), block)

    own = blk(me)
    others = partners(me, count)

    for copy in loads:
        copy.wait()

    def wide(row):
        return jnp.transpose(jnp.broadcast_to(row, (128, 128)))

    @pl.loop(0, rows // 128)
    def _(j):
        at = pl.ds(pl.multiple_of(j * 128, 128), 128)
        scale = 1.0 / (wide(virt_rows[pl.ds(j, 1), :]) + occ_own[...])
        scale_a[at, :] = scale
        start_a[at, :] = s_buf[at, :] * scale

    pl.semaphore_wait(barrier, count - 1 + 2)

    edge_rows = REACH * VT

    def send_edges(k, ref):
        for side, (first, where) in enumerate(((0, down), (rows - edge_rows, up))):
            base = (1 - side) * edge_rows
            pltpu.make_async_remote_copy(
                src_ref=ref.at[pl.ds(first, edge_rows)],
                dst_ref=halo.at[k, pl.ds(base, edge_rows)],
                send_sem=edge_sem.at[k, side],
                recv_sem=halo_sem.at[k, side],
                device_id={"sec": where},
                device_id_type=MESH,
            ).start()

    def wait_edges(k, ref, what):
        for side, (first, where) in enumerate(((0, down), (rows - edge_rows, up))):
            base = (1 - side) * edge_rows
            copy = pltpu.make_async_remote_copy(
                src_ref=ref.at[pl.ds(first, edge_rows)],
                dst_ref=halo.at[k, pl.ds(base, edge_rows)],
                send_sem=edge_sem.at[k, side],
                recv_sem=halo_sem.at[k, side],
                device_id={"sec": where},
                device_id_type=MESH,
            )
            if what == "recv":
                copy.wait_recv()
            else:
                copy.wait_send()

    def send_blocks(phase, src, dst):
        for d in others:
            pltpu.make_async_remote_copy(
                src_ref=src.at[blk(d)],
                dst_ref=dst.at[own],
                send_sem=send_sem.at[phase],
                recv_sem=recv_sem.at[phase],
                device_id={"pair": d},
                device_id_type=MESH,
            ).start()

    def wait_blocks(phase, src, dst, what):
        all_but_one = pl.ds(0, rows - block)
        copy = pltpu.make_async_remote_copy(
            src_ref=src.at[all_but_one],
            dst_ref=dst.at[all_but_one],
            send_sem=send_sem.at[phase],
            recv_sem=recv_sem.at[phase],
            device_id={"pair": others[0]},
            device_id_type=MESH,
        )
        if what == "recv":
            copy.wait_recv()
        else:
            copy.wait_send()

    send_edges(0, start_a)
    for d in others:
        pltpu.make_async_remote_copy(
            src_ref=occ_own,
            dst_ref=occ_all.at[me],
            send_sem=occ_sem.at[0],
            recv_sem=occ_sem.at[1],
            device_id={"pair": d},
            device_id_type=MESH,
        ).start()
    send_blocks(0, start_a, start_b)
    occ_all[pl.ds(me, 1)] = occ_own[...].reshape(1, 1, 128)
    start_b[own, :] = start_a[own, :]

    def put_window(at, values):
        high, low = split(values)
        window[at, 0:128] = high
        window[at, 128:256] = low

    def put_halo(k):
        for side in range(2):
            for i in range(REACH):
                src = pl.ds(side * edge_rows + i * VT, VT)
                first = i * VT if side == 0 else (REACH + section + i) * VT
                put_window(pl.ds(first, VT), halo[k, src, :])

    @pl.loop(0, section)
    def _(i):
        put_window(
            pl.ds(pl.multiple_of((i + REACH) * VT, VT), VT),
            start_a[pl.ds(pl.multiple_of(i * VT, VT), VT), :],
        )

    for g in range(groups):
        v_loads[g].wait()

        @pl.loop(g * per_group, (g + 1) * per_group)
        def _(n):
            tile = jnp.transpose(v_stage[pl.ds(pl.multiple_of(n * VT, VT), VT), :])
            before = prev_v[n]
            for half in range(2):
                total = tile[half * 128 : half * 128 + 128, :]
                total = total + v_split[before, half, 0:128, :].astype(F32)
                total = total + v_split[before, half, 128:256, :].astype(F32)
                high, low = split(total)
                v_split[n, half, 0:128, :] = high
                v_split[n, half, 128:256, :] = low

    def particle(dst):
        @pl.loop(0, section)
        def _(c):
            slab = window[pl.ds(pl.multiple_of(c * VT, VT), SPAN * VT), :]
            for half in range(2):
                tiles = []
                for o in range(SPAN):
                    tiles.append(v_split[last_v[c * SPAN + o], half])
                product = jnp.dot(
                    jnp.concatenate(tiles, axis=1), slab, preferred_element_type=F32
                )
                both = product[:, 0:128] + product[:, 128:256]
                to = pl.ds(pl.multiple_of(c * VT + half * 128, 128), 128)
                dst[to, :] = both[0:128, :] + both[128:256, :]

    wait_edges(0, start_a, "recv")
    put_halo(0)
    particle(part_a.at[0])
    send_blocks(1, part_a.at[0], part_b.at[0])
    part_b[0, own, :] = part_a[0, own, :]

    w_load.wait()

    @pl.loop(0, wslots)
    def _(n):
        tile = jnp.transpose(w_stage[pl.ds(pl.multiple_of(n * OT, OT), OT), :])
        high, low = split(tile)
        for k in range(2):
            at = pl.ds(pl.multiple_of(n * 2 * OT + k * OT, OT), OT)
            w_split[at, 0:128] = high
            w_split[at, 128:256] = low

    my_virt = virt_rows[pl.ds(lax.div(me * block, 128), 1), :] if block < 128 else None
    if block < 128:
        virt_wide[pl.ds(0, 128), :] = wide(my_virt)
        first = pl.multiple_of(lax.rem(me * block, 128), block)
    else:
        for j in range(block // 128):
            virt_wide[pl.ds(j * 128, 128), :] = wide(
                virt_rows[pl.ds(me * (block // 128) + j, 1), :]
            )
        first = 0

    def put_split(q, values):
        high, low = split(values)
        split_b[q, :, 0:128] = high
        split_b[q, :, 128:256] = low

    def hole(dst):
        @pl.loop(0, wslots)
        def _(n):
            weight = w_split[pl.ds(pl.multiple_of(n * 2 * OT, 2 * OT), 2 * OT), :]
            product = jnp.dot(split_b[w_cols[n]], weight, preferred_element_type=F32)
            chain[n] = product[:, 0:128] + product[:, 128:256] + chain[prev_w[n]]

        @pl.loop(0, count)
        def _(r):
            dst[blk(r), :] = chain[last_w[r]]

    pltpu.make_async_remote_copy(
        src_ref=occ_all.at[pl.ds(0, count - 1)],
        dst_ref=occ_all.at[pl.ds(0, count - 1)],
        send_sem=occ_sem.at[0],
        recv_sem=occ_sem.at[1],
        device_id={"pair": others[0]},
        device_id_type=MESH,
    ).wait_recv()
    wait_blocks(0, start_a, start_b, "recv")

    @pl.loop(0, count)
    def _(q):
        at = blk(q)
        row = occ_all[pl.ds(q, 1)].reshape(1, 128)
        scale_b[at, :] = 1.0 / (virt_wide[pl.ds(first, block), :] + row)
        put_split(q, start_b[at, :])

    hole(hole_b.at[0])
    send_blocks(2, hole_b.at[0], hole_a.at[0])
    hole_a[0, own, :] = hole_b[0, own, :]

    def advance_b(k):
        @pl.loop(0, count)
        def _(q):
            at = blk(q)
            put_split(q, start_b[at, :] + (part_b[k, at, :] + hole_b[k, at, :]) * scale_b[at, :])

    def advance_a(k):
        for i in list(range(REACH)) + list(range(section - REACH, section)):
            at = pl.ds(i * VT, VT)
            edge[k, at, :] = (
                start_a[at, :] + (part_a[k, at, :] + hole_a[k, at, :]) * scale_a[at, :]
            )
        send_edges(k + 1, edge.at[k])
        for i in list(range(REACH)) + list(range(section - REACH, section)):
            put_window(pl.ds((i + REACH) * VT, VT), edge[k, pl.ds(i * VT, VT), :])

        @pl.loop(REACH, section - REACH)
        def _(i):
            at = pl.ds(pl.multiple_of(i * VT, VT), VT)
            put_window(
                pl.ds(pl.multiple_of((i + REACH) * VT, VT), VT),
                start_a[at, :] + (part_a[k, at, :] + hole_a[k, at, :]) * scale_a[at, :],
            )

        wait_edges(k + 1, edge.at[k], "recv")
        put_halo(k + 1)

    wait_blocks(1, part_a.at[0], part_b.at[0], "recv")
    advance_b(0)
    hole(hole_b.at[1])
    send_blocks(3, hole_b.at[1], hole_a.at[1])
    hole_a[1, own, :] = hole_b[1, own, :]

    wait_blocks(2, hole_b.at[0], hole_a.at[0], "recv")
    advance_a(0)
    particle(part_a.at[1])
    send_blocks(4, part_a.at[1], part_b.at[1])
    part_b[1, own, :] = part_a[1, own, :]

    wait_blocks(3, hole_b.at[1], hole_a.at[1], "recv")
    advance_a(1)
    particle(part_a.at[2])

    wait_blocks(4, part_a.at[1], part_b.at[1], "recv")
    advance_b(1)
    hole(hole_b.at[2])
    send_blocks(5, hole_b.at[2], hole_a.at[2])
    hole_a[2, own, :] = hole_b[2, own, :]

    wait_blocks(5, hole_b.at[2], hole_a.at[2], "recv")

    @pl.loop(0, section)
    def _(i):
        at = pl.ds(pl.multiple_of(i * VT, VT), VT)
        s_buf[at, :] = start_a[at, :] + (part_a[2, at, :] + hole_a[2, at, :]) * scale_a[at, :]

    store = pltpu.make_async_copy(s_buf, out, load_sem.at[0])
    store.start()
    pltpu.make_async_remote_copy(
        src_ref=occ_all.at[pl.ds(0, count - 1)],
        dst_ref=occ_all.at[pl.ds(0, count - 1)],
        send_sem=occ_sem.at[0],
        recv_sem=occ_sem.at[1],
        device_id={"pair": others[0]},
        device_id_type=MESH,
    ).wait_send()
    wait_blocks(0, start_a, start_b, "send")
    wait_blocks(1, part_a.at[0], part_b.at[0], "send")
    wait_blocks(2, hole_b.at[0], hole_a.at[0], "send")
    wait_blocks(3, hole_b.at[1], hole_a.at[1], "send")
    wait_blocks(4, part_a.at[1], part_b.at[1], "send")
    wait_blocks(5, hole_b.at[2], hole_a.at[2], "send")
    wait_edges(0, start_a, "send")
    wait_edges(1, edge.at[0], "send")
    wait_edges(2, edge.at[1], "send")
    store.wait()


def local(
    count,
    sections,
    source,
    occ_energy,
    virt_energy,
    v_tiles,
    v_rows,
    v_cols,
    v_count,
    w_tiles,
    w_rows,
    w_cols,
):
    rows = source.shape[0]
    block = rows // count
    section = rows // VT
    slots, wslots = v_tiles.shape[0], w_tiles.shape[0]
    lists = tables(v_rows, v_cols, v_count, w_rows, section, count)
    smem = pl.BlockSpec(memory_space=pltpu.SMEM)
    hbm = pl.BlockSpec(memory_space=pl.ANY)
    vmem = pltpu.VMEM
    dma = pltpu.SemaphoreType.DMA
    whole = vmem((rows, 128), F32)
    return pl.pallas_call(
        functools.partial(kernel, count, sections),
        out_shape=jax.ShapeDtypeStruct((rows, 128), F32),
        in_specs=[smem] * 5 + [hbm] * 5,
        out_specs=hbm,
        scratch_shapes=[
            whole,
            vmem((1, 128), F32),
            vmem((count, 1, 128), F32),
            vmem((rows // 128, 128), F32),
            vmem((max(block, 128), 128), F32),
            vmem((slots * VT, VT), F32),
            vmem((wslots * OT, OT), F32),
            vmem((slots + 1, 2, VT, VT), BF16),
            vmem((wslots * 2 * OT, 2 * OT), BF16),
            whole,
            whole,
            whole,
            whole,
            vmem((3, rows, 128), F32),
            vmem((2, rows, 128), F32),
            vmem((3, rows, 128), F32),
            vmem((3, rows, 128), F32),
            vmem(((section + 2 * REACH) * VT, 256), BF16),
            vmem((count, block, 256), BF16),
            vmem((wslots + 1, block, 128), F32),
            vmem((2, rows, 128), F32),
            vmem((3, 2 * REACH * VT, 128), F32),
            dma((4,)),
            dma((4,)),
            dma((2,)),
            dma((6,)),
            dma((6,)),
            dma((3, 2)),
            dma((3, 2)),
        ],
        compiler_params=pltpu.CompilerParams(
            collective_id=0, has_side_effects=True, vmem_limit_bytes=62 * 1024 * 1024
        ),
        name="ladders",
    )(
        *lists,
        w_cols,
        source,
        occ_energy.reshape(1, 128),
        virt_energy.reshape(rows // 128, 128),
        v_tiles.reshape(slots * VT, VT),
        w_tiles.reshape(wslots * OT, OT),
    )


def solution(mesh):
    in_specs = (
        P("sec", "pair"),
        P("pair"),
        P("sec"),
        P("sec", None, None),
        P("sec"),
        P("sec"),
        P("sec"),
        P(),
        P(),
        P(),
    )
    body = functools.partial(local, mesh.shape["pair"], mesh.shape["sec"])
    return jax.shard_map(
        body, mesh=mesh, in_specs=in_specs, out_specs=P("sec", "pair"), check_vma=False
    )
```

profile of v0, /device:TPU:1, one launch (start us, length us, event | category | flops | bytes accessed | tf_op | source)
XLA Modules:
  0.0 113.6 jit_solution(16351156492173876798)
XLA Ops:
  0.7 2.5 %tables.1 = (s32[40]{0:T(128)}, s32[32]{0:T(128)}, s32[32]{0:T(128)}, s32[48]{0:T(128)}) custom-call(s32[32]{0:T(128)} %v_rows.1, s32[32]{0:T(128)} %v_cols.1, s32[1]{0:T(128)S(6)} %copy.12.v_count, s32[48]{0:T(128)} %w_rows.1), custom_call_target="tpu_custom_call" | custom-call | tf_op jit(solution)/shard_map/tables/pallas_call | solution.py:57
  3.1 108.2 %ladders.1 = f32[2048,128]{1,0:T(8,128)} custom-call(s32[40]{0:T(128)} %get-tuple-element.9.last_v, s32[32]{0:T(128)} %get-tuple-element.10.prev_v, s32[32]{0:T(128)} %get-tuple-element.11.last_w, s32[48]{0:T(128)} %get-tuple-element.12.prev_w, s32[48]{0:T(128)} %w_cols.1, f32[2048,128]{1,0:T(8,128)} %source.1, f32[1,128]{1,0:T(1,128)} %bitcast.7, ...), custom_call_target="tpu_custom_call" | custom-call | tf_op jit(solution)/shard_map/ladders/pallas_call | solution.py:473
  111.3 2.3 %copy.13 = f32[2048,128]{1,0:T(8,128)} copy(f32[2048,128]{1,0:T(8,128)} %ladders.1) | data formatting | bytes 2097152
where the time goes:
time: 114 us
  Pallas kernels  111 us (97%)
  local copies, waits for them, and re-layouts  2.26 us (2%)
    pallas_call x1, Pallas kernels, local(): pl.pallas_call(functools.partial(kernel, count, sections), out_shape=jax....  108 us
    pallas_call x1, Pallas kernels, tables(): pl.pallas_call(tables_kernel, out_shape=(i32(section * SPAN), i32(v_rows....  2.45 us

commit v1 on v0

v1 whole, which is shorter than its diff:
```python
import functools

import jax
import jax.numpy as jnp
from jax import lax
from jax.experimental import pallas as pl
from jax.experimental.pallas import tpu as pltpu
from jax.sharding import PartitionSpec as P

MESH = pl.DeviceIdType.MESH
VT = 256
OT = 128
REACH = 2
SPAN = 2 * REACH + 1
F32 = jnp.float32
BF16 = jnp.bfloat16
UNROLL = 8
VMEM_LIMIT = 62 * 1024 * 1024


def split(x):
    high = x.astype(BF16)
    low = (x - high.astype(F32)).astype(BF16)
    return high, low


def last_match(keys, queries, depth, earlier):
    column = jnp.transpose(jnp.broadcast_to(keys, (128, 128)))[0:depth, :]
    n = lax.broadcasted_iota(jnp.int32, (depth, 128), 0)
    match = column == queries
    if earlier:
        match = match & (n < lax.broadcasted_iota(jnp.int32, (depth, 128), 1))
    found = jnp.max(jnp.where(match, n, -1), axis=0, keepdims=True)
    return jnp.where(found < 0, depth, found)


def far_first():
    steps = [(dx, dy, dc) for dx in range(-1, 3) for dy in range(-1, 3) for dc in range(2)]
    steps.remove((0, 0, 0))
    return sorted(steps, key=lambda s: -abs(s[0]) - abs(s[1]))


def partners(me, count):
    if count != 32:
        return [lax.rem(me + k, count) for k in range(1, count)]
    y, x, c = lax.div(me, 8), lax.rem(lax.div(me, 2), 4), lax.rem(me, 2)
    return [
        lax.rem(y + dy + 4, 4) * 8 + lax.rem(x + dx + 4, 4) * 2 + lax.rem(c + dc, 2)
        for dx, dy, dc in far_first()
    ]


def kernel(
    count,
    sections,
    v_count,
    w_cols,
    v_rows,
    v_cols,
    w_rows,
    source,
    occ,
    virt,
    v_tiles,
    w_tiles,
    out,
    s_buf,
    occ_own,
    occ_all,
    virt_rows,
    virt_wide,
    v_row,
    v_col,
    w_row,
    keys,
    table,
    index,
    v_stage,
    w_stage,
    v_split,
    w_split,
    start_a,
    scale_a,
    start_b,
    scale_b,
    part_a,
    part_b,
    hole_b,
    hole_a,
    window,
    split_b,
    chain,
    edge,
    halo,
    load_sem,
    list_sem,
    v_sem,
    occ_sem,
    send_sem,
    recv_sem,
    edge_sem,
    halo_sem,
    store_sem,
):
    rows = source.shape[0]
    block = rows // count
    half = block // 2
    section = rows // VT
    slots = v_tiles.shape[0] // VT
    wslots = w_tiles.shape[0] // OT
    groups = v_sem.shape[0]
    per_group = slots // groups
    me = lax.axis_index("pair")
    z = lax.axis_index("sec")
    up, down = lax.rem(z + 1, sections), lax.rem(z + sections - 1, sections)

    loads = [
        pltpu.make_async_copy(occ, occ_own, load_sem.at[1]),
        pltpu.make_async_copy(virt, virt_rows, load_sem.at[2]),
        pltpu.make_async_copy(source, s_buf, load_sem.at[0]),
    ]
    for copy in loads:
        copy.start()
    list_loads = [
        pltpu.make_async_copy(v_rows, v_row, list_sem.at[0]),
        pltpu.make_async_copy(v_cols, v_col, list_sem.at[1]),
        pltpu.make_async_copy(w_rows, w_row, list_sem.at[2]),
    ]
    for copy in list_loads:
        copy.start()
    v_loads = []
    for g in range(groups):
        part = pl.ds(g * per_group * VT, per_group * VT)
        v_loads.append(pltpu.make_async_copy(v_tiles.at[part], v_stage.at[part], v_sem.at[g]))
        v_loads[-1].start()
    w_load = pltpu.make_async_copy(w_tiles, w_stage, load_sem.at[3])
    w_load.start()

    barrier = pltpu.get_barrier_semaphore()

    @pl.loop(1, count)
    def _(k):
        pl.semaphore_signal(
            barrier, inc=1, device_id={"pair": lax.rem(me + k, count)}, device_id_type=MESH
        )

    pl.semaphore_signal(barrier, inc=1, device_id={"sec": up}, device_id_type=MESH)
    pl.semaphore_signal(barrier, inc=1, device_id={"sec": down}, device_id_type=MESH)

    def blk(d):
        return pl.ds(pl.multiple_of(d * block, block), block)

    def piece(d, part, parts):
        size = block // parts
        return pl.ds(pl.multiple_of(d * block + part * size, size), size)

    own = blk(me)
    others = partners(me, count)

    for copy in loads:
        copy.wait()

    def wide(row):
        return jnp.transpose(jnp.broadcast_to(row, (128, 128)))

    @pl.loop(0, rows // 128, unroll=4)
    def _(j):
        at = pl.ds(pl.multiple_of(j * 128, 128), 128)
        scale = 1.0 / (wide(virt_rows[pl.ds(j, 1), :]) + occ_own[...])
        scale_a[at, :] = scale
        start_a[at, :] = s_buf[at, :] * scale

    pl.semaphore_wait(barrier, count - 1 + 2)

    edge_rows = REACH * VT

    def edge_copies(k, ref):
        return [
            pltpu.make_async_remote_copy(
                src_ref=ref.at[pl.ds(first, edge_rows)],
                dst_ref=halo.at[k, pl.ds((1 - side) * edge_rows, edge_rows)],
                send_sem=edge_sem.at[k, side],
                recv_sem=halo_sem.at[k, side],
                device_id={"sec": where},
                device_id_type=MESH,
            )
            for side, (first, where) in enumerate(((0, down), (rows - edge_rows, up)))
        ]

    def send_edges(k, ref):
        for copy in edge_copies(k, ref):
            copy.start()

    def wait_edges(k, ref):
        for copy in edge_copies(k, ref):
            copy.wait_recv()

    def send_blocks(phase, src, dst, part=0, parts=1):
        for d in others:
            pltpu.make_async_remote_copy(
                src_ref=src.at[piece(d, part, parts)],
                dst_ref=dst.at[piece(me, part, parts)],
                send_sem=send_sem.at[phase],
                recv_sem=recv_sem.at[phase],
                device_id={"pair": d},
                device_id_type=MESH,
            ).start()

    def all_blocks(phase, src, dst, parts=1):
        all_but_one = pl.ds(0, (rows - block) // parts)
        return pltpu.make_async_remote_copy(
            src_ref=src.at[all_but_one],
            dst_ref=dst.at[all_but_one],
            send_sem=send_sem.at[phase],
            recv_sem=recv_sem.at[phase],
            device_id={"pair": others[0]},
            device_id_type=MESH,
        )

    all_occ = pltpu.make_async_remote_copy(
        src_ref=occ_all.at[pl.ds(0, count - 1)],
        dst_ref=occ_all.at[pl.ds(0, count - 1)],
        send_sem=occ_sem.at[0],
        recv_sem=occ_sem.at[1],
        device_id={"pair": others[0]},
        device_id_type=MESH,
    )

    send_edges(0, start_a)
    send_blocks(0, start_a, start_b)
    for d in others:
        pltpu.make_async_remote_copy(
            src_ref=occ_own,
            dst_ref=occ_all.at[me],
            send_sem=occ_sem.at[0],
            recv_sem=occ_sem.at[1],
            device_id={"pair": d},
            device_id_type=MESH,
        ).start()
    occ_all[pl.ds(me, 1)] = occ_own[...].reshape(1, 1, 128)
    start_b[own, :] = start_a[own, :]

    for copy in list_loads:
        copy.wait()
    lane = lax.broadcasted_iota(jnp.int32, (1, 128), 1)
    keys[...] = jnp.full((2, 128), -1, jnp.int32)
    listed = v_col[...] * SPAN + v_row[...] - v_col[...]
    keys[0:1, 0:slots] = jnp.where(lane[:, 0:slots] < v_count[0], listed, -1)
    keys[1:2, 0:wslots] = w_row[...]
    v_key, w_key = keys[0:1, :], keys[1:2, :]
    table[0:1, :] = last_match(v_key, lane, slots, False)
    table[1:2, :] = last_match(v_key, v_key, slots, True)
    table[2:3, :] = last_match(w_key, lane, wslots, False)
    table[3:4, :] = last_match(w_key, w_key, wslots, True)
    to_index = pltpu.make_async_copy(table, index, list_sem.at[3])
    to_index.start()

    def put_window(at, values):
        high, low = split(values)
        window[at, 0:128] = high
        window[at, 128:256] = low

    def put_halo(k):
        for i in range(2 * REACH):
            first = i * VT if i < REACH else (section + i) * VT
            put_window(pl.ds(first, VT), halo[k, pl.ds(i * VT, VT), :])

    @pl.loop(0, section)
    def _(i):
        put_window(
            pl.ds(pl.multiple_of((i + REACH) * VT, VT), VT),
            start_a[pl.ds(pl.multiple_of(i * VT, VT), VT), :],
        )

    v_split[slots] = jnp.zeros((2 * VT, VT), BF16)
    chain[wslots] = jnp.zeros((block, OT), F32)
    to_index.wait()

    for g in range(groups):
        v_loads[g].wait()

        @pl.loop(g * per_group, (g + 1) * per_group)
        def _(n):
            tile = jnp.transpose(v_stage[pl.ds(pl.multiple_of(n * VT, VT), VT), :])
            before = index[1, n]
            total = tile + v_split[before, 0:VT, :].astype(F32)
            total = total + v_split[before, VT : 2 * VT, :].astype(F32)
            high, low = split(total)
            v_split[n, 0:VT, :] = high
            v_split[n, VT : 2 * VT, :] = low

    def particle(dst, first, last):
        @pl.loop(first, last)
        def _(c):
            slab = window[pl.ds(pl.multiple_of(c * VT, VT), SPAN * VT), :]
            tiles = [v_split[index[0, c * SPAN + o]] for o in range(SPAN)]
            product = jnp.dot(jnp.concatenate(tiles, axis=1), slab, preferred_element_type=F32)
            both = product[:, 0:128] + product[:, 128:256]
            dst[pl.ds(pl.multiple_of(c * VT, VT), VT), :] = both[0:VT, :] + both[VT : 2 * VT, :]

    def particle_ends(k, ref, dst):
        wait_edges(k, ref)
        put_halo(k)
        particle(dst, 0, REACH)
        particle(dst, section - REACH, section)

    w_load.wait()

    @pl.loop(0, wslots, unroll=2)
    def _(n):
        tile = jnp.transpose(w_stage[pl.ds(pl.multiple_of(n * OT, OT), OT), :])
        high, low = split(tile)
        w_split[n, :, 0:128] = high
        w_split[n, :, 128:256] = low

    particle(part_a.at[0], REACH, section - REACH)
    particle_ends(0, start_a, part_a.at[0])
    send_blocks(1, part_a.at[0], part_b.at[0])
    part_b[0, own, :] = part_a[0, own, :]

    per_row = max(block // 128, 1)
    for j in range(per_row):
        row = lax.div(me * block, 128) + j
        virt_wide[pl.ds(j * 128, 128), :] = wide(virt_rows[pl.ds(row, 1), :])
    first = pl.multiple_of(lax.rem(me * block, 128), block) if block < 128 else 0

    def put_split(q, values, part):
        high, low = split(values)
        split_b[part, q, 0:half, :] = high
        split_b[part, q, half:block, :] = low

    def hole(dst, parts):
        size = len(parts) * half
        to = pl.ds(parts[0] * half, size)

        @pl.loop(0, wslots, step=UNROLL)
        def _(n0):
            sums = []
            for k in range(UNROLL):
                n = n0 + k
                at = w_cols[n]
                left = [split_b[part, at] for part in parts]
                left = left[0] if len(left) == 1 else jnp.concatenate(left, axis=0)
                product = jnp.dot(left, w_split[n], preferred_element_type=F32)
                both = product[:, 0:128] + product[:, 128:256]
                both = [
                    both[i * block : i * block + half] + both[i * block + half : (i + 1) * block]
                    for i in range(len(parts))
                ]
                sums.append(both[0] if len(both) == 1 else jnp.concatenate(both, axis=0))
            for k in range(UNROLL):
                chain[n0 + k, to, :] = sums[k] + chain[index[3, n0 + k], to, :]

        @pl.loop(0, count, unroll=4)
        def _(r):
            at = pl.ds(pl.multiple_of(r * block + parts[0] * half, half), size)
            dst[at, :] = chain[index[2, r], to, :]

    all_occ.wait_recv()

    @pl.loop(0, count, unroll=4)
    def _(q):
        row = occ_all[pl.ds(q, 1)].reshape(1, 128)
        scale_b[blk(q), :] = 1.0 / (virt_wide[pl.ds(first, block), :] + row)

    all_blocks(0, start_a, start_b).wait_recv()

    @pl.loop(0, count, unroll=4)
    def _(q):
        for part in range(2):
            put_split(q, start_b[piece(q, part, 2), :], part)

    hole(hole_b.at[0], (0, 1))
    send_blocks(2, hole_b.at[0], hole_a.at[0])
    hole_a[0, own, :] = hole_b[0, own, :]

    def advance_b(k, parts):
        @pl.loop(0, count, unroll=4)
        def _(q):
            for part in parts:
                at = piece(q, part, 2)
                change = (part_b[k, at, :] + hole_b[k, at, :]) * scale_b[at, :]
                put_split(q, start_b[at, :] + change, part)

    ends = list(range(REACH)) + list(range(section - REACH, section))

    def advance_a(k):
        def moved(at):
            return start_a[at, :] + (part_a[k, at, :] + hole_a[k, at, :]) * scale_a[at, :]

        for i in ends:
            at = pl.ds(i * VT, VT)
            edge[k, at, :] = moved(at)
        send_edges(k + 1, edge.at[k])
        for i in ends:
            put_window(pl.ds((i + REACH) * VT, VT), edge[k, pl.ds(i * VT, VT), :])

        @pl.loop(REACH, section - REACH)
        def _(i):
            at = pl.ds(pl.multiple_of(i * VT, VT), VT)
            put_window(pl.ds(pl.multiple_of((i + REACH) * VT, VT), VT), moved(at))

        particle(part_a.at[k + 1], REACH, section - REACH)
        particle_ends(k + 1, edge.at[k], part_a.at[k + 1])

    all_blocks(1, part_a.at[0], part_b.at[0]).wait_recv()
    advance_b(0, (0, 1))
    hole(hole_b.at[1], (0, 1))
    send_blocks(3, hole_b.at[1], hole_a.at[1])
    hole_a[1, own, :] = hole_b[1, own, :]

    all_blocks(2, hole_b.at[0], hole_a.at[0]).wait_recv()
    advance_a(0)
    for part in range(2):
        send_blocks(4 + part, part_a.at[1], part_b.at[1], part, 2)
    part_b[1, own, :] = part_a[1, own, :]

    all_blocks(3, hole_b.at[1], hole_a.at[1]).wait_recv()
    advance_a(1)

    for part in range(2):
        all_blocks(4 + part, part_a.at[1], part_b.at[1], 2).wait_recv()
        advance_b(1, (part,))
        hole(hole_b.at[2], (part,))
        send_blocks(6 + part, hole_b.at[2], hole_a.at[2], part, 2)
    hole_a[2, own, :] = hole_b[2, own, :]

    @pl.loop(0, section)
    def _(i):
        at = pl.ds(pl.multiple_of(i * VT, VT), VT)
        s_buf[at, :] = start_a[at, :] + part_a[2, at, :] * scale_a[at, :]

    for part in range(2):
        all_blocks(6 + part, hole_b.at[2], hole_a.at[2], 2).wait_recv()
    stores = []
    for i in range(section):
        at = pl.ds(i * VT, VT)
        s_buf[at, :] = s_buf[at, :] + hole_a[2, at, :] * scale_a[at, :]
        stores.append(pltpu.make_async_copy(s_buf.at[at], out.at[at], store_sem.at[i]))
        stores[-1].start()

    all_occ.wait_send()
    all_blocks(0, start_a, start_b).wait_send()
    all_blocks(1, part_a.at[0], part_b.at[0]).wait_send()
    all_blocks(2, hole_b.at[0], hole_a.at[0]).wait_send()
    all_blocks(3, hole_b.at[1], hole_a.at[1]).wait_send()
    for part in range(2):
        all_blocks(4 + part, part_a.at[1], part_b.at[1], 2).wait_send()
        all_blocks(6 + part, hole_b.at[2], hole_a.at[2], 2).wait_send()
    for k, ref in enumerate((start_a, edge.at[0], edge.at[1])):
        for copy in edge_copies(k, ref):
            copy.wait_send()
    for copy in stores:
        copy.wait()


def local(
    count,
    sections,
    source,
    occ_energy,
    virt_energy,
    v_tiles,
    v_rows,
    v_cols,
    v_count,
    w_tiles,
    w_rows,
    w_cols,
):
    rows = source.shape[0]
    block = rows // count
    section = rows // VT
    slots, wslots = v_tiles.shape[0], w_tiles.shape[0]
    smem = pl.BlockSpec(memory_space=pltpu.SMEM)
    hbm = pl.BlockSpec(memory_space=pl.ANY)
    vmem = pltpu.VMEM
    dma = pltpu.SemaphoreType.DMA
    whole = vmem((rows, 128), F32)
    return pl.pallas_call(
        functools.partial(kernel, count, sections),
        out_shape=jax.ShapeDtypeStruct((rows, 128), F32),
        in_specs=[smem] * 2 + [hbm] * 8,
        out_specs=hbm,
        scratch_shapes=[
            whole,
            vmem((1, 128), F32),
            vmem((count, 1, 128), F32),
            vmem((rows // 128, 128), F32),
            vmem((max(block, 128), 128), F32),
            vmem((1, slots), jnp.int32),
            vmem((1, slots), jnp.int32),
            vmem((1, wslots), jnp.int32),
            vmem((2, 128), jnp.int32),
            vmem((8, 128), jnp.int32),
            pltpu.SMEM((8, 128), jnp.int32),
            vmem((slots * VT, VT), F32),
            vmem((wslots * OT, OT), F32),
            vmem((slots + 1, 2 * VT, VT), BF16),
            vmem((wslots, OT, 2 * OT), BF16),
            whole,
            whole,
            whole,
            whole,
            vmem((3, rows, 128), F32),
            vmem((2, rows, 128), F32),
            vmem((3, rows, 128), F32),
            vmem((3, rows, 128), F32),
            vmem(((section + 2 * REACH) * VT, 256), BF16),
            vmem((2, count, block, 128), BF16),
            vmem((wslots + 1, block, 128), F32),
            vmem((2, rows, 128), F32),
            vmem((3, 2 * REACH * VT, 128), F32),
            dma((4,)),
            dma((4,)),
            dma((4,)),
            dma((2,)),
            dma((8,)),
            dma((8,)),
            dma((3, 2)),
            dma((3, 2)),
            dma((section,)),
        ],
        compiler_params=pltpu.CompilerParams(
            collective_id=0, has_side_effects=True, vmem_limit_bytes=VMEM_LIMIT
        ),
        name="ladders",
    )(
        v_count,
        w_cols,
        v_rows.reshape(1, slots),
        v_cols.reshape(1, slots),
        w_rows.reshape(1, wslots),
        source,
        occ_energy.reshape(1, 128),
        virt_energy.reshape(rows // 128, 128),
        v_tiles.reshape(slots * VT, VT),
        w_tiles.reshape(wslots * OT, OT),
    )


def solution(mesh):
    in_specs = (
        P("sec", "pair"),
        P("pair"),
        P("sec"),
        P("sec", None, None),
        P("sec"),
        P("sec"),
        P("sec"),
        P(),
        P(),
        P(),
    )
    body = functools.partial(local, mesh.shape["pair"], mesh.shape["sec"])
    return jax.shard_map(
        body, mesh=mesh, in_specs=in_specs, out_specs=P("sec", "pair"), check_vma=False
    )
```

time: 114 us -> 91.8 us (0.81)
  Pallas kernels: 111 us -> 88.7 us
    pallas_call x1, Pallas kernels: 108 us -> 88.7 us  [local(): pl.pallas_call(functools.partial(kernel, count, sections), out_shape=jax....]
    pallas_call x1 -> x0, Pallas kernels: 2.45 us -> none  [tables(): pl.pallas_call(tables_kernel, out_shape=(i32(section * SPAN), i32(v_rows....]
where the time goes in v1:
time: 91.8 us; the launch traced here: 91.6 us
  Pallas kernels  88.7 us (97%)
  local copies, waits for them, and re-layouts  2.26 us (2%)
    pallas_call x1, Pallas kernels, local(): pl.pallas_call(functools.partial(kernel, count, sections), out_shape=jax....  88.7 us
    unnamed x1, local copies, waits for them, and re-layouts  2.26 us

profile of v1, /device:TPU:1, one launch (start us, length us, event | category | flops | bytes accessed | tf_op | source)
XLA Modules:
  0.0 91.6 jit_solution(5405950335189073503)
XLA Ops:
  0.7 88.7 %ladders.1 = f32[2048,128]{1,0:T(8,128)} custom-call(s32[1]{0:T(128)S(6)} %copy.12.v_count, s32[48]{0:T(128)} %w_cols.1, s32[1,32]{1,0:T(1,128)} %bitcast.10, s32[1,32]{1,0:T(1,128)} %bitcast.11, s32[1,48]{1,0:T(1,128)} %bitcast.12, f32[2048,128]{1,0:T(8,128)} %source.1, f32[1,128]{1,0:T(1,128)} %bitcast.13, f32[16,128]{1,0:T(8,128)} %bitcast.9, ...), custom_call_target="tpu_custom_call" | custom-call | tf_op jit(solution)/shard_map/ladders/pallas_call | solution.py:480
  89.4 2.3 %copy.13 = f32[2048,128]{1,0:T(8,128)} copy(f32[2048,128]{1,0:T(8,128)} %ladders.1) | data formatting | bytes 2097152

commit v2 on v1

v2 whole, which is shorter than its diff:
```python
import functools

import jax
import jax.numpy as jnp
from jax import lax
from jax.experimental import pallas as pl
from jax.experimental.pallas import tpu as pltpu
from jax.sharding import PartitionSpec as P

MESH = pl.DeviceIdType.MESH
VT = 256
OT = 128
REACH = 2
SPAN = 2 * REACH + 1
F32 = jnp.float32
BF16 = jnp.bfloat16
UNROLL = 8
VMEM_LIMIT = 52 * 1024 * 1024


def split(x):
    high = x.astype(BF16)
    low = (x - high.astype(F32)).astype(BF16)
    return high, low


def last_match(keys, queries, depth, earlier):
    column = jnp.transpose(jnp.broadcast_to(keys, (128, 128)))[0:depth, :]
    n = lax.broadcasted_iota(jnp.int32, (depth, 128), 0)
    match = column == queries
    if earlier:
        match = match & (n < lax.broadcasted_iota(jnp.int32, (depth, 128), 1))
    found = jnp.max(jnp.where(match, n, -1), axis=0, keepdims=True)
    return jnp.where(found < 0, depth, found)


def far_first():
    steps = [(dx, dy, dc) for dx in range(-1, 3) for dy in range(-1, 3) for dc in range(2)]
    steps.remove((0, 0, 0))
    return sorted(steps, key=lambda s: -abs(s[0]) - abs(s[1]))


def partners(me, count):
    if count != 32:
        return [lax.rem(me + k, count) for k in range(1, count)]
    y, x, c = lax.div(me, 8), lax.rem(lax.div(me, 2), 4), lax.rem(me, 2)
    return [
        lax.rem(y + dy + 4, 4) * 8 + lax.rem(x + dx + 4, 4) * 2 + lax.rem(c + dc, 2)
        for dx, dy, dc in far_first()
    ]


def kernel(
    count,
    sections,
    v_count,
    w_cols,
    v_rows,
    v_cols,
    w_rows,
    source,
    occ,
    virt,
    v_tiles,
    w_tiles,
    out,
    s_buf,
    occ_own,
    occ_all,
    virt_rows,
    virt_wide,
    virt_b,
    v_row,
    v_col,
    w_row,
    keys,
    table,
    index,
    v_stage,
    w_stage,
    v_split,
    w_split,
    start_a,
    scale_a,
    start_b,
    scale_b,
    part_a,
    part_b,
    hole_b,
    hole_a,
    window,
    split_b,
    chain,
    edge,
    halo,
    load_sem,
    list_sem,
    v_sem,
    occ_sem,
    send_sem,
    recv_sem,
    edge_sem,
    halo_sem,
):
    section = source.shape[0]
    strip = VT // count
    block = section * strip
    half = block // 2
    slots_half = section // 2
    slots = v_tiles.shape[0] // VT
    wslots = w_tiles.shape[0] // OT
    groups = v_sem.shape[0]
    per_group = slots // groups
    me = lax.axis_index("pair")
    z = lax.axis_index("sec")
    up, down = lax.rem(z + 1, sections), lax.rem(z + sections - 1, sections)

    barrier = pltpu.get_barrier_semaphore()

    @pl.loop(1, count)
    def _(k):
        pl.semaphore_signal(
            barrier, inc=1, device_id={"pair": lax.rem(me + k, count)}, device_id_type=MESH
        )

    pl.semaphore_signal(barrier, inc=1, device_id={"sec": up}, device_id_type=MESH)
    pl.semaphore_signal(barrier, inc=1, device_id={"sec": down}, device_id_type=MESH)

    loads = [
        pltpu.make_async_copy(occ, occ_own, load_sem.at[1]),
        pltpu.make_async_copy(virt, virt_rows, load_sem.at[2]),
        pltpu.make_async_copy(source, s_buf, load_sem.at[0]),
    ]
    for copy in loads:
        copy.start()
    list_loads = [
        pltpu.make_async_copy(v_rows, v_row, list_sem.at[0]),
        pltpu.make_async_copy(v_cols, v_col, list_sem.at[1]),
        pltpu.make_async_copy(w_rows, w_row, list_sem.at[2]),
    ]
    for copy in list_loads:
        copy.start()
    v_loads = []
    for g in range(groups):
        part = pl.ds(g * per_group * VT, per_group * VT)
        v_loads.append(pltpu.make_async_copy(v_tiles.at[part], v_stage.at[part], v_sem.at[g]))
        v_loads[-1].start()
    w_load = pltpu.make_async_copy(w_tiles, w_stage, load_sem.at[3])
    w_load.start()

    inner = [(REACH, 0, section - 2 * REACH)]
    outer = [(0, slots_half, REACH), (section - REACH, slots_half + REACH, REACH)]
    spans = (inner, outer)
    tile_of_slot = [t + i for span in spans for t, _, n in span for i in range(n)]

    def strips(d):
        return pl.ds(pl.multiple_of(d * strip, strip), strip)

    def piece(q, part):
        return pl.ds(q * section + part * slots_half, slots_half)

    others = partners(me, count)

    def send(phase, part, src, dst, back):
        for d in others:
            for tile, slot, n in spans[part]:
                if back:
                    from_ = src.at[pl.ds(d * section + slot, n)]
                    to = dst.at[pl.ds(tile, n), strips(me)]
                else:
                    from_ = src.at[pl.ds(tile, n), strips(d)]
                    to = dst.at[pl.ds(me * section + slot, n)]
                pltpu.make_async_remote_copy(
                    src_ref=from_,
                    dst_ref=to,
                    send_sem=send_sem.at[phase, part],
                    recv_sem=recv_sem.at[phase, part],
                    device_id={"pair": d},
                    device_id_type=MESH,
                ).start()

    def keep(src, dst, back):
        for slot, tile in enumerate(tile_of_slot):
            if back:
                dst[tile, strips(me), :] = src[me * section + slot]
            else:
                dst[me * section + slot] = src[tile, strips(me), :]

    def all_of(phase, part, dst):
        some = dst.at[pl.ds(0, (count - 1) * slots_half)]
        return pltpu.make_async_remote_copy(
            src_ref=some,
            dst_ref=some,
            send_sem=send_sem.at[phase, part],
            recv_sem=recv_sem.at[phase, part],
            device_id={"pair": others[0]},
            device_id_type=MESH,
        )

    def as_strips(ref):
        return ref.reshape(count * section, strip, 128)

    all_occ = pltpu.make_async_remote_copy(
        src_ref=occ_all.at[pl.ds(0, count - 1)],
        dst_ref=occ_all.at[pl.ds(0, count - 1)],
        send_sem=occ_sem.at[0],
        recv_sem=occ_sem.at[1],
        device_id={"pair": others[0]},
        device_id_type=MESH,
    )

    pl.semaphore_wait(barrier, count - 1 + 2)
    for part in range(2):
        send(0, part, source, start_b, False)
    for d in others:
        pltpu.make_async_remote_copy(
            src_ref=occ,
            dst_ref=occ_all.at[me],
            send_sem=occ_sem.at[0],
            recv_sem=occ_sem.at[1],
            device_id={"pair": d},
            device_id_type=MESH,
        ).start()

    for copy in loads:
        copy.wait()

    def wide(row):
        return jnp.transpose(jnp.broadcast_to(row, (128, 128)))

    @pl.loop(0, section, unroll=2)
    def _(i):
        for j in range(VT // 128):
            at = pl.ds(j * 128, 128)
            virt_row = virt_rows[pl.ds(i * (VT // 128) + j, 1), :]
            scale = 1.0 / (wide(virt_row) + occ_own[...])
            scale_a[i, at, :] = scale
            start_a[i, at, :] = s_buf[i, at, :] * scale

    def edge_copies(k, ref):
        return [
            pltpu.make_async_remote_copy(
                src_ref=ref.at[pl.ds(first, REACH)],
                dst_ref=halo.at[k, pl.ds((1 - side) * REACH, REACH)],
                send_sem=edge_sem.at[k, side],
                recv_sem=halo_sem.at[k, side],
                device_id={"sec": where},
                device_id_type=MESH,
            )
            for side, (first, where) in enumerate(((0, down), (section - REACH, up)))
        ]

    def send_edges(k, ref):
        for copy in edge_copies(k, ref):
            copy.start()

    def wait_edges(k, ref):
        for copy in edge_copies(k, ref):
            copy.wait_recv()

    send_edges(0, start_a)
    occ_all[pl.ds(me, 1)] = occ_own[...].reshape(1, 1, 128)
    keep(s_buf, start_b, False)

    for copy in list_loads:
        copy.wait()
    lane = lax.broadcasted_iota(jnp.int32, (1, 128), 1)
    keys[...] = jnp.full((2, 128), -1, jnp.int32)
    listed = v_col[...] * SPAN + v_row[...] - v_col[...]
    keys[0:1, 0:slots] = jnp.where(lane[:, 0:slots] < v_count[0], listed, -1)
    keys[1:2, 0:wslots] = w_row[...]
    v_key, w_key = keys[0:1, :], keys[1:2, :]
    table[0:1, :] = last_match(v_key, lane, slots, False)
    table[1:2, :] = last_match(v_key, v_key, slots, True)
    table[2:3, :] = last_match(w_key, lane, wslots, False)
    table[3:4, :] = last_match(w_key, w_key, wslots, True)
    to_index = pltpu.make_async_copy(table, index, list_sem.at[3])
    to_index.start()

    def put_window(i, values):
        high, low = split(values)
        at = pl.ds(pl.multiple_of(i * VT, VT), VT)
        window[at, 0:128] = high
        window[at, 128:256] = low

    def put_halo(k):
        for i in range(2 * REACH):
            put_window(i if i < REACH else section + i, halo[k, i])

    @pl.loop(0, section)
    def _(i):
        put_window(i + REACH, start_a[i])

    v_split[slots] = jnp.zeros((2 * VT, VT), BF16)
    chain[wslots] = jnp.zeros((block, OT), F32)
    to_index.wait()

    for g in range(groups):
        v_loads[g].wait()

        @pl.loop(g * per_group, (g + 1) * per_group)
        def _(n):
            tile = jnp.transpose(v_stage[pl.ds(pl.multiple_of(n * VT, VT), VT), :])
            before = index[1, n]
            total = tile + v_split[before, 0:VT, :].astype(F32)
            total = total + v_split[before, VT : 2 * VT, :].astype(F32)
            high, low = split(total)
            v_split[n, 0:VT, :] = high
            v_split[n, VT : 2 * VT, :] = low

    def particle(dst, first, last):
        @pl.loop(first, last)
        def _(c):
            slab = window[pl.ds(pl.multiple_of(c * VT, VT), SPAN * VT), :]
            tiles = [v_split[index[0, c * SPAN + o]] for o in range(SPAN)]
            product = jnp.dot(jnp.concatenate(tiles, axis=1), slab, preferred_element_type=F32)
            both = product[:, 0:128] + product[:, 128:256]
            dst[c] = both[0:VT, :] + both[VT : 2 * VT, :]

    def particle_ends(k, ref, dst):
        wait_edges(k, ref)
        put_halo(k)
        particle(dst, 0, REACH)
        particle(dst, section - REACH, section)

    particle(part_a.at[0], REACH, section - REACH)
    send(1, 0, part_a.at[0], part_b.at[0], False)
    particle_ends(0, start_a, part_a.at[0])
    send(1, 1, part_a.at[0], part_b.at[0], False)
    keep(part_a.at[0], part_b.at[0], False)

    w_load.wait()

    @pl.loop(0, wslots, unroll=2)
    def _(n):
        tile = jnp.transpose(w_stage[pl.ds(pl.multiple_of(n * OT, OT), OT), :])
        high, low = split(tile)
        w_split[n, :, 0:128] = high
        w_split[n, :, 128:256] = low

    for slot, tile in enumerate(tile_of_slot):
        row = tile * (VT // 128) + lax.div(me * strip, 128)
        virt_wide[...] = wide(virt_rows[pl.ds(row, 1), :])
        first = pl.multiple_of(lax.rem(me * strip, 128), strip)
        virt_b[slot] = virt_wide[pl.ds(first, strip), :]

    def put_split(q, values, part):
        high, low = split(values)
        split_b[part, q, 0:half, :] = high
        split_b[part, q, half:block, :] = low

    def hole(dst, parts):
        size = len(parts) * half
        to = pl.ds(parts[0] * half, size)

        @pl.loop(0, wslots, step=UNROLL)
        def _(n0):
            sums = []
            for k in range(UNROLL):
                n = n0 + k
                at = w_cols[n]
                left = [split_b[part, at] for part in parts]
                left = left[0] if len(left) == 1 else jnp.concatenate(left, axis=0)
                product = jnp.dot(left, w_split[n], preferred_element_type=F32)
                both = product[:, 0:128] + product[:, 128:256]
                both = [
                    both[i * block : i * block + half] + both[i * block + half : (i + 1) * block]
                    for i in range(len(parts))
                ]
                sums.append(both[0] if len(both) == 1 else jnp.concatenate(both, axis=0))
            for k in range(UNROLL):
                chain[n0 + k, to, :] = sums[k] + chain[index[3, n0 + k], to, :]

        @pl.loop(0, count, unroll=4)
        def _(r):
            at = pl.ds(r * section + parts[0] * slots_half, len(parts) * slots_half)
            dst[at] = chain[index[2, r], to, :].reshape(len(parts) * slots_half, strip, 128)

    all_occ.wait_recv()

    @pl.loop(0, count, unroll=4)
    def _(q):
        row = occ_all[pl.ds(q, 1)].reshape(1, 1, 128)
        scale_b[pl.ds(q * section, section)] = 1.0 / (virt_b[...] + row)

    for part in range(2):
        all_of(0, part, start_b).wait_recv()

    @pl.loop(0, count, unroll=4)
    def _(q):
        for part in range(2):
            at = piece(q, part)
            start = start_b[at] * scale_b[at]
            start_b[at] = start
            put_split(q, start.reshape(half, 128), part)

    hole(hole_b.at[0], (0, 1))
    for part in (1, 0):
        send(2, part, hole_b.at[0], hole_a.at[0], True)
    keep(hole_b.at[0], hole_a.at[0], True)

    def advance_b(k, parts):
        @pl.loop(0, count, unroll=4)
        def _(q):
            for part in parts:
                at = piece(q, part)
                change = (part_b[k, at] + hole_b[k, at]) * scale_b[at]
                put_split(q, (start_b[at] + change).reshape(half, 128), part)

    ends = list(range(REACH)) + list(range(section - REACH, section))

    def advance_a(k, phase):
        def moved(i):
            return start_a[i] + (part_a[k, i] + hole_a[k, i]) * scale_a[i]

        all_of(phase, 1, as_strips(hole_a.at[k])).wait_recv()
        for i in ends:
            edge[k, i] = moved(i)
        send_edges(k + 1, edge.at[k])
        for i in ends:
            put_window(i + REACH, edge[k, i])
        all_of(phase, 0, as_strips(hole_a.at[k])).wait_recv()

        @pl.loop(REACH, section - REACH)
        def _(i):
            put_window(i + REACH, moved(i))

        particle(part_a.at[k + 1], REACH, section - REACH)

    for part in range(2):
        all_of(1, part, part_b.at[0]).wait_recv()
        advance_b(0, (part,))
    hole(hole_b.at[1], (0, 1))
    for part in (1, 0):
        send(3, part, hole_b.at[1], hole_a.at[1], True)
    keep(hole_b.at[1], hole_a.at[1], True)

    advance_a(0, 2)
    send(4, 0, part_a.at[1], part_b.at[1], False)
    particle_ends(1, edge.at[0], part_a.at[1])
    send(4, 1, part_a.at[1], part_b.at[1], False)
    keep(part_a.at[1], part_b.at[1], False)

    advance_a(1, 3)

    for part in range(2):
        all_of(4, part, part_b.at[1]).wait_recv()
        advance_b(1, (part,))
        hole(hole_b.at[2], (part,))
        send(5, part, hole_b.at[2], hole_a.at[2], True)
    keep(hole_b.at[2], hole_a.at[2], True)
    particle_ends(2, edge.at[1], part_a.at[2])

    @pl.loop(0, section)
    def _(i):
        s_buf[i] = start_a[i] + part_a[2, i] * scale_a[i]

    for part in range(2):
        all_of(5, part, as_strips(hole_a.at[2])).wait_recv()
        for tile, _, n in spans[part]:

            @pl.loop(tile, tile + n)
            def _(i):
                out[i] = s_buf[i] + hole_a[2, i] * scale_a[i]

    all_occ.wait_send()
    for phase in range(6):
        for part in range(2):
            all_of(phase, part, start_b).wait_send()
    for k, ref in enumerate((start_a, edge.at[0], edge.at[1])):
        for copy in edge_copies(k, ref):
            copy.wait_send()


def local(
    count,
    sections,
    source,
    occ_energy,
    virt_energy,
    v_tiles,
    v_rows,
    v_cols,
    v_count,
    w_tiles,
    w_rows,
    w_cols,
):
    rows = source.shape[0]
    block = rows // count
    section = rows // VT
    strip = VT // count
    slots, wslots = v_tiles.shape[0], w_tiles.shape[0]
    smem = pl.BlockSpec(memory_space=pltpu.SMEM)
    hbm = pl.BlockSpec(memory_space=pl.ANY)
    vmem = pltpu.VMEM
    dma = pltpu.SemaphoreType.DMA
    whole = vmem((section, VT, 128), F32)
    turned = vmem((count * section, strip, 128), F32)
    return pl.pallas_call(
        functools.partial(kernel, count, sections),
        out_shape=jax.ShapeDtypeStruct((section, VT, 128), F32),
        in_specs=[smem] * 2 + [hbm] * 8,
        out_specs=pl.BlockSpec(memory_space=pltpu.VMEM),
        scratch_shapes=[
            whole,
            vmem((1, 128), F32),
            vmem((count, 1, 128), F32),
            vmem((rows // 128, 128), F32),
            vmem((128, 128), F32),
            vmem((section, strip, 128), F32),
            vmem((1, slots), jnp.int32),
            vmem((1, slots), jnp.int32),
            vmem((1, wslots), jnp.int32),
            vmem((2, 128), jnp.int32),
            vmem((8, 128), jnp.int32),
            pltpu.SMEM((8, 128), jnp.int32),
            vmem((slots * VT, VT), F32),
            vmem((wslots * OT, OT), F32),
            vmem((slots + 1, 2 * VT, VT), BF16),
            vmem((wslots, OT, 2 * OT), BF16),
            whole,
            whole,
            turned,
            turned,
            vmem((3, section, VT, 128), F32),
            vmem((2, count * section, strip, 128), F32),
            vmem((3, count * section, strip, 128), F32),
            vmem((3, section, VT, 128), F32),
            vmem(((section + 2 * REACH) * VT, 256), BF16),
            vmem((2, count, block, 128), BF16),
            vmem((wslots + 1, block, 128), F32),
            vmem((2, section, VT, 128), F32),
            vmem((3, 2 * REACH, VT, 128), F32),
            dma((4,)),
            dma((4,)),
            dma((4,)),
            dma((2,)),
            dma((6, 2)),
            dma((6, 2)),
            dma((3, 2)),
            dma((3, 2)),
        ],
        compiler_params=pltpu.CompilerParams(
            collective_id=0, has_side_effects=True, vmem_limit_bytes=VMEM_LIMIT
        ),
        name="ladders",
    )(
        v_count,
        w_cols,
        v_rows.reshape(1, slots),
        v_cols.reshape(1, slots),
        w_rows.reshape(1, wslots),
        source.reshape(section, VT, 128),
        occ_energy.reshape(1, 128),
        virt_energy.reshape(rows // 128, 128),
        v_tiles.reshape(slots * VT, VT),
        w_tiles.reshape(wslots * OT, OT),
    ).reshape(rows, 128)


def solution(mesh):
    in_specs = (
        P("sec", "pair"),
        P("pair"),
        P("sec"),
        P("sec", None, None),
        P("sec"),
        P("sec"),
        P("sec"),
        P(),
        P(),
        P(),
    )
    body = functools.partial(local, mesh.shape["pair"], mesh.shape["sec"])
    return jax.shard_map(
        body, mesh=mesh, in_specs=in_specs, out_specs=P("sec", "pair"), check_vma=False
    )
```

time: 91.8 us -> 87.2 us (0.950)
  Pallas kernels: 88.7 us -> 81.4 us
  local copies, waits for them, and re-layouts: 2.26 us -> 4.94 us
    pallas_call x1, Pallas kernels: 88.7 us -> 81.4 us  [local(): pl.pallas_call(functools.partial(kernel, count, sections), out_shape=jax....]
    unnamed x1 -> x13, local copies, waits for them, and re-layouts: 2.26 us -> 4.94 us
where the time goes in v2:
time: 87.2 us; the launch traced here: 87 us
  Pallas kernels  81.4 us (93%)
  local copies, waits for them, and re-layouts  4.94 us (6%)
    pallas_call x1, Pallas kernels, local(): pl.pallas_call(functools.partial(kernel, count, sections), out_shape=jax....  81.4 us
    unnamed x13, local copies, waits for them, and re-layouts  4.94 us

profile of v2, /device:TPU:1, one launch (start us, length us, event | category | flops | bytes accessed | tf_op | source)
XLA Modules:
  0.0 87.0 jit_solution(17719539869298971620)
XLA Ops:
  0.7 0.0 copy-start
  0.7 0.7 copy-done
  1.4 0.0 copy-start.1
  1.4 0.7 copy-done.1
  2.0 0.0 copy-start.2
  2.0 0.7 copy-done.2
  2.7 0.0 copy-start.3
  2.7 0.7 copy-done.3
  3.3 0.0 copy-start.4
  3.3 0.7 copy-done.4
  4.0 0.0 copy-start.5
  4.0 0.7 copy-done.5
  4.6 81.4 %ladders.1 = f32[8,256,128]{2,1,0:T(8,128)S(1)} custom-call(s32[1]{0:T(128)S(6)} %copy.12.v_count, s32[48]{0:T(128)S(1)} %copy-done.1, s32[1,32]{1,0:T(1,128)S(1)} %bitcast.11, s32[1,32]{1,0:T(1,128)S(1)} %bitcast.12, s32[1,48]{1,0:T(1,128)S(1)} %bitcast.13, f32[8,256,128]{2,1,0:T(8,128)} %bitcast.17, f32[1,128]{1,0:T(1,128)S(1)} %bitcast.14, ...), custom_call_target="tpu_custom_call" | custom-call | tf_op jit(solution)/shard_map/ladders/pallas_call | solution.py:500
  86.0 1.0 %copy.13 = f32[2048,128]{1,0:T(8,128)} copy(f32[2048,128]{1,0:T(8,128)S(1)} %bitcast.9) | data formatting | bytes 2097152
Async XLA Ops:
  0.7 0.7 copy-start
  1.4 0.7 copy-start.1
  2.0 0.7 copy-start.2
  2.7 0.7 copy-start.3
  3.3 0.7 copy-start.4
  4.0 0.7 copy-start.5

commit v3 on v2

--- a/solution.py
+++ b/solution.py
@@ -15,7 +15,7 @@
 F32 = jnp.float32
 BF16 = jnp.bfloat16
 UNROLL = 8
-VMEM_LIMIT = 52 * 1024 * 1024
+VMEM_LIMIT = 62 * 1024 * 1024
 
 
 def split(x):
@@ -54,10 +54,10 @@
     count,
     sections,
     v_count,
-    w_cols,
     v_rows,
     v_cols,
     w_rows,
+    w_cols,
     source,
     occ,
     virt,
@@ -73,6 +73,7 @@
     v_row,
     v_col,
     w_row,
+    w_col,
     keys,
     table,
     index,
@@ -101,6 +102,7 @@
     recv_sem,
     edge_sem,
     halo_sem,
+    store_sem,
 ):
     section = source.shape[0]
     strip = VT // count
@@ -137,6 +139,7 @@
         pltpu.make_async_copy(v_rows, v_row, list_sem.at[0]),
         pltpu.make_async_copy(v_cols, v_col, list_sem.at[1]),
         pltpu.make_async_copy(w_rows, w_row, list_sem.at[2]),
+        pltpu.make_async_copy(w_cols, w_col, list_sem.at[4]),
     ]
     for copy in list_loads:
         copy.start()
@@ -270,10 +273,12 @@
     keys[0:1, 0:slots] = jnp.where(lane[:, 0:slots] < v_count[0], listed, -1)
     keys[1:2, 0:wslots] = w_row[...]
     v_key, w_key = keys[0:1, :], keys[1:2, :]
+    table[...] = jnp.zeros((8, 128), jnp.int32)
     table[0:1, :] = last_match(v_key, lane, slots, False)
     table[1:2, :] = last_match(v_key, v_key, slots, True)
     table[2:3, :] = last_match(w_key, lane, wslots, False)
     table[3:4, :] = last_match(w_key, w_key, wslots, True)
+    table[4:5, 0:wslots] = w_col[...]
     to_index = pltpu.make_async_copy(table, index, list_sem.at[3])
     to_index.start()
 
@@ -358,7 +363,7 @@
             sums = []
             for k in range(UNROLL):
                 n = n0 + k
-                at = w_cols[n]
+                at = index[4, n]
                 left = [split_b[part, at] for part in parts]
                 left = left[0] if len(left) == 1 else jnp.concatenate(left, axis=0)
                 product = jnp.dot(left, w_split[n], preferred_element_type=F32)
@@ -455,13 +460,14 @@
     def _(i):
         s_buf[i] = start_a[i] + part_a[2, i] * scale_a[i]
 
+    stores = []
     for part in range(2):
         all_of(5, part, as_strips(hole_a.at[2])).wait_recv()
         for tile, _, n in spans[part]:
-
-            @pl.loop(tile, tile + n)
-            def _(i):
-                out[i] = s_buf[i] + hole_a[2, i] * scale_a[i]
+            for i in range(tile, tile + n):
+                s_buf[i] = s_buf[i] + hole_a[2, i] * scale_a[i]
+                stores.append(pltpu.make_async_copy(s_buf.at[i], out.at[i], store_sem.at[i]))
+                stores[-1].start()
 
     all_occ.wait_send()
     for phase in range(6):
@@ -470,6 +476,8 @@
     for k, ref in enumerate((start_a, edge.at[0], edge.at[1])):
         for copy in edge_copies(k, ref):
             copy.wait_send()
+    for copy in stores:
+        copy.wait()
 
 
 def local(
@@ -491,7 +499,6 @@
     section = rows // VT
     strip = VT // count
     slots, wslots = v_tiles.shape[0], w_tiles.shape[0]
-    smem = pl.BlockSpec(memory_space=pltpu.SMEM)
     hbm = pl.BlockSpec(memory_space=pl.ANY)
     vmem = pltpu.VMEM
     dma = pltpu.SemaphoreType.DMA
@@ -500,8 +507,8 @@
     return pl.pallas_call(
         functools.partial(kernel, count, sections),
         out_shape=jax.ShapeDtypeStruct((section, VT, 128), F32),
-        in_specs=[smem] * 2 + [hbm] * 8,
-        out_specs=pl.BlockSpec(memory_space=pltpu.VMEM),
+        in_specs=[pl.BlockSpec(memory_space=pltpu.SMEM)] + [hbm] * 9,
+        out_specs=hbm,
         scratch_shapes=[
             whole,
             vmem((1, 128), F32),
@@ -511,6 +518,7 @@
             vmem((section, strip, 128), F32),
             vmem((1, slots), jnp.int32),
             vmem((1, slots), jnp.int32),
+            vmem((1, wslots), jnp.int32),
             vmem((1, wslots), jnp.int32),
             vmem((2, 128), jnp.int32),
             vmem((8, 128), jnp.int32),
@@ -533,13 +541,14 @@
             vmem((2, section, VT, 128), F32),
             vmem((3, 2 * REACH, VT, 128), F32),
             dma((4,)),
-            dma((4,)),
+            dma((5,)),
             dma((4,)),
             dma((2,)),
             dma((6, 2)),
             dma((6, 2)),
             dma((3, 2)),
             dma((3, 2)),
+            dma((section,)),
         ],
         compiler_params=pltpu.CompilerParams(
             collective_id=0, has_side_effects=True, vmem_limit_bytes=VMEM_LIMIT
@@ -547,10 +556,10 @@
         name="ladders",
     )(
         v_count,
-        w_cols,
         v_rows.reshape(1, slots),
         v_cols.reshape(1, slots),
         w_rows.reshape(1, wslots),
+        w_cols.reshape(1, wslots),
         source.reshape(section, VT, 128),
         occ_energy.reshape(1, 128),
         virt_energy.reshape(rows // 128, 128),

time: 87.2 us -> 84.8 us (0.972)
  local copies, waits for them, and re-layouts: 4.94 us -> 2.26 us
    unnamed x13 -> x1, local copies, waits for them, and re-layouts: 4.94 us -> 2.26 us
where the time goes in v3:
time: 84.8 us; the launch traced here: 84.7 us
  Pallas kernels  81.8 us (96%)
  local copies, waits for them, and re-layouts  2.26 us (3%)
    pallas_call x1, Pallas kernels, local(): pl.pallas_call(functools.partial(kernel, count, sections), out_shape=jax....  81.8 us
    unnamed x1, local copies, waits for them, and re-layouts  2.26 us

profile of v3, /device:TPU:1, one launch (start us, length us, event | category | flops | bytes accessed | tf_op | source)
XLA Modules:
  0.0 84.7 jit_solution(8141986709845861469)
XLA Ops:
  0.7 81.8 %ladders.1 = f32[8,256,128]{2,1,0:T(8,128)} custom-call(s32[1]{0:T(128)S(6)} %copy.12.v_count, s32[1,32]{1,0:T(1,128)} %bitcast.15, s32[1,32]{1,0:T(1,128)} %bitcast.16, s32[1,48]{1,0:T(1,128)} %bitcast.17, s32[1,48]{1,0:T(1,128)} %bitcast.18, f32[8,256,128]{2,1,0:T(8,128)} %bitcast.13, f32[1,128]{1,0:T(1,128)} %bitcast.19, f32[16,128]{1,0:T(8,128)} %bitcast.14, ...), custom_call_target="tpu_custom_call" | custom-call | tf_op jit(solution)/shard_map/ladders/pallas_call | solution.py:507
  82.5 2.3 %copy.13 = f32[2048,128]{1,0:T(8,128)} copy(f32[2048,128]{1,0:T(8,128)} %bitcast.11) | data formatting | bytes 2097152

commit v4 on v3

--- a/solution.py
+++ b/solution.py
@@ -63,7 +63,8 @@
     virt,
     v_tiles,
     w_tiles,
-    out,
+    base_out,
+    change_out,
     s_buf,
     occ_own,
     occ_all,
@@ -354,7 +355,7 @@
         split_b[part, q, 0:half, :] = high
         split_b[part, q, half:block, :] = low
 
-    def hole(dst, parts):
+    def hole(dst, parts, scaled=False):
         size = len(parts) * half
         to = pl.ds(parts[0] * half, size)
 
@@ -379,7 +380,8 @@
         @pl.loop(0, count, unroll=4)
         def _(r):
             at = pl.ds(r * section + parts[0] * slots_half, len(parts) * slots_half)
-            dst[at] = chain[index[2, r], to, :].reshape(len(parts) * slots_half, strip, 128)
+            total = chain[index[2, r], to, :].reshape(len(parts) * slots_half, strip, 128)
+            dst[at] = total * scale_b[at] if scaled else total
 
     all_occ.wait_recv()
 
@@ -451,23 +453,28 @@
     for part in range(2):
         all_of(4, part, part_b.at[1]).wait_recv()
         advance_b(1, (part,))
-        hole(hole_b.at[2], (part,))
-        send(5, part, hole_b.at[2], hole_a.at[2], True)
-    keep(hole_b.at[2], hole_a.at[2], True)
+        hole(hole_b.at[2], (part,), True)
+        send(5, part, hole_b.at[2], change_out, True)
+    stores = []
+    for tile, slot, n in inner + outer:
+        stores.append(
+            pltpu.make_async_copy(
+                hole_b.at[2, pl.ds(me * section + slot, n)],
+                change_out.at[pl.ds(tile, n), strips(me)],
+                store_sem.at[len(stores)],
+            )
+        )
+        stores[-1].start()
     particle_ends(2, edge.at[1], part_a.at[2])
 
     @pl.loop(0, section)
     def _(i):
         s_buf[i] = start_a[i] + part_a[2, i] * scale_a[i]
 
-    stores = []
+    stores.append(pltpu.make_async_copy(s_buf, base_out, store_sem.at[len(stores)]))
+    stores[-1].start()
     for part in range(2):
-        all_of(5, part, as_strips(hole_a.at[2])).wait_recv()
-        for tile, _, n in spans[part]:
-            for i in range(tile, tile + n):
-                s_buf[i] = s_buf[i] + hole_a[2, i] * scale_a[i]
-                stores.append(pltpu.make_async_copy(s_buf.at[i], out.at[i], store_sem.at[i]))
-                stores[-1].start()
+        all_of(5, part, as_strips(change_out)).wait_recv()
 
     all_occ.wait_send()
     for phase in range(6):
@@ -478,6 +485,38 @@
             copy.wait_send()
     for copy in stores:
         copy.wait()
+
+
+def join_kernel(base, change, out, base_buf, change_buf, out_buf, base_sem, change_sem, out_sem):
+    pieces = range(base.shape[0])
+    loads = []
+    for i in pieces:
+        loads.append(pltpu.make_async_copy(base.at[i], base_buf.at[i], base_sem.at[i]))
+        loads.append(pltpu.make_async_copy(change.at[i], change_buf.at[i], change_sem.at[i]))
+    for copy in loads:
+        copy.start()
+    stores = [pltpu.make_async_copy(out_buf.at[i], out.at[i], out_sem.at[i]) for i in pieces]
+    for i in pieces:
+        loads[2 * i].wait()
+        loads[2 * i + 1].wait()
+        out_buf[i] = base_buf[i] + change_buf[i]
+        stores[i].start()
+    for copy in stores:
+        copy.wait()
+
+
+def join(base, change):
+    hbm = pl.BlockSpec(memory_space=pl.ANY)
+    return pl.pallas_call(
+        join_kernel,
+        out_shape=jax.ShapeDtypeStruct(base.shape, base.dtype),
+        in_specs=[hbm] * 2,
+        out_specs=hbm,
+        scratch_shapes=[pltpu.VMEM(base.shape, base.dtype)] * 3
+        + [pltpu.SemaphoreType.DMA((base.shape[0],))] * 3,
+        compiler_params=pltpu.CompilerParams(vmem_limit_bytes=VMEM_LIMIT),
+        name="join",
+    )(base, change)
 
 
 def local(
@@ -504,11 +543,11 @@
     dma = pltpu.SemaphoreType.DMA
     whole = vmem((section, VT, 128), F32)
     turned = vmem((count * section, strip, 128), F32)
-    return pl.pallas_call(
+    base, change = pl.pallas_call(
         functools.partial(kernel, count, sections),
-        out_shape=jax.ShapeDtypeStruct((section, VT, 128), F32),
+        out_shape=(jax.ShapeDtypeStruct((section, VT, 128), F32),) * 2,
         in_specs=[pl.BlockSpec(memory_space=pltpu.SMEM)] + [hbm] * 9,
-        out_specs=hbm,
+        out_specs=(hbm, hbm),
         scratch_shapes=[
             whole,
             vmem((1, 128), F32),
@@ -534,7 +573,7 @@
             vmem((3, section, VT, 128), F32),
             vmem((2, count * section, strip, 128), F32),
             vmem((3, count * section, strip, 128), F32),
-            vmem((3, section, VT, 128), F32),
+            vmem((2, section, VT, 128), F32),
             vmem(((section + 2 * REACH) * VT, 256), BF16),
             vmem((2, count, block, 128), BF16),
             vmem((wslots + 1, block, 128), F32),
@@ -548,7 +587,7 @@
             dma((6, 2)),
             dma((3, 2)),
             dma((3, 2)),
-            dma((section,)),
+            dma((4,)),
         ],
         compiler_params=pltpu.CompilerParams(
             collective_id=0, has_side_effects=True, vmem_limit_bytes=VMEM_LIMIT
@@ -565,7 +604,8 @@
         virt_energy.reshape(rows // 128, 128),
         v_tiles.reshape(slots * VT, VT),
         w_tiles.reshape(wslots * OT, OT),
-    ).reshape(rows, 128)
+    )
+    return join(base, change).reshape(rows, 128)
 
 
 def solution(mesh):

time: 84.8 us -> 84.3 us (level)
  local copies, waits for them, and re-layouts: 2.26 us -> 0 us
  Pallas kernels: 81.8 us -> 83.6 us
    unnamed x1 -> x0, local copies, waits for them, and re-layouts: 2.26 us -> none
    pallas_call x1 -> x2, Pallas kernels: 81.8 us -> 83.6 us  [the longest x1 81.1 us: local(): pl.pallas_call(functools.partial(kernel, count, sections), out_shape=(jax...]
where the time goes in v4:
time: 84.3 us; the launch traced here: 84.2 us
  Pallas kernels  83.6 us (99%)
    pallas_call x1, Pallas kernels, local(): pl.pallas_call(functools.partial(kernel, count, sections), out_shape=(jax...  81.1 us
    pallas_call x1, Pallas kernels, join(): pl.pallas_call(join_kernel, out_shape=jax.ShapeDtypeStruct(base.shape, ba...  2.48 us

profile of v4, /device:TPU:1, one launch (start us, length us, event | category | flops | bytes accessed | tf_op | source)
XLA Modules:
  0.0 84.2 jit_solution(15640699152572860844)
XLA Ops:
  0.7 81.1 %ladders.1 = (f32[8,256,128]{2,1,0:T(8,128)}, f32[8,256,128]{2,1,0:T(8,128)}) custom-call(s32[1]{0:T(128)S(6)} %copy.11.v_count, s32[1,32]{1,0:T(1,128)} %bitcast.14, s32[1,32]{1,0:T(1,128)} %bitcast.15, s32[1,48]{1,0:T(1,128)} %bitcast.16, s32[1,48]{1,0:T(1,128)} %bitcast.17, f32[8,256,128]{2,1,0:T(8,128)} %bitcast.12, f32[1,128]{1,0:T(1,128)} %bitcast.18, ...), custom_call_target="tpu_custom_call" | custom-call | tf_op jit(solution)/shard_map/ladders/pallas_call | solution.py:546
  81.7 2.5 %join.1 = f32[8,256,128]{2,1,0:T(8,128)} custom-call(f32[8,256,128]{2,1,0:T(8,128)} %get-tuple-element.7.base, f32[8,256,128]{2,1,0:T(8,128)} %get-tuple-element.8.change), custom_call_target="tpu_custom_call" | custom-call | tf_op jit(solution)/shard_map/join/pallas_call | solution.py:510
